TPU v7x, 256 devices: a whole 4x4x8 slice. The times are simulated.
256 devices in a mesh: segment: 8 (over x, y_hi), dp: 32 (over y_lo, z, core).
Axes of the slice: x: 4, y: 4 (y_hi: 2, y_lo: 2; y = y_hi * 2 + y_lo), z: 8, core: 2. Of those that a mesh axis runs over, the one named last changes fastest.
Arguments:
- encoder_patch_input: bfloat16 [32, 1024, 1024], P('dp'), may hold values from -6 to 6
- encoder_norm_gains: float32 [8, 1024], P('segment'), may hold values from 0.5 to 1.5
- encoder_input_weight: bfloat16 [8, 1024, 2048], P('segment'), may hold values from -0.1875 to 0.1875
- encoder_output_weight: bfloat16 [8, 2048, 1024], P('segment'), may hold values from -0.125 to 0.125
- diffuser_hidden_states: bfloat16 [32, 1024, 2048], P('dp', 'segment'), may hold values from -6 to 6
- projector_first_weight: bfloat16 [2048, 2048], P('dp', 'segment'), may hold values from -0.125 to 0.125
- projector_second_weight: bfloat16 [2048, 1024], P(('segment', 'dp')), may hold values from -0.125 to 0.125
Outputs:
- grad_w1: float32 [2048, 2048], P('dp', 'segment')
- grad_w2: float32 [2048, 1024], P(('segment', 'dp'))
All inputs are finite; a program needn't handle non-finite values.
Results may differ from a plain program's by a relative error of at most 0.014.
Values may be sent and summed in bfloat16 or wider, within the bound.
A program may use at most 128 MiB of HBM per device.

v0:
```python
import jax
import jax.numpy as jnp
from jax import lax
from jax.sharding import PartitionSpec as P

norm_eps = 1e-06


def shifted(block, axis, distance):
    devices = range(lax.axis_size(axis))
    route = [(i - distance, i) for i in devices if i - distance in devices]
    return lax.ppermute(block, axis, route)


def from_root(block, axis, holder):
    block = jnp.where(lax.axis_index(axis) == holder, block, jnp.zeros_like(block))
    return lax.psum(block, axis)


def encoder_layer(hidden, scale_row, weight_in, weight_out):
    floats = hidden.astype(jnp.float32)
    normed = (
        floats * lax.rsqrt(jnp.mean(floats * floats, axis=-1, keepdims=True) + norm_eps) * scale_row
    )
    inner = jnp.dot(normed.astype(jnp.bfloat16), weight_in, preferred_element_type=jnp.float32)
    inner = jax.nn.gelu(inner, approximate=True).astype(jnp.bfloat16)
    return (floats + jnp.dot(inner, weight_out, preferred_element_type=jnp.float32)).astype(
        jnp.bfloat16
    )


def cosine_grad(projected, features):
    feat_f = features.astype(jnp.float32)
    squared = jnp.sum(projected * projected, axis=-1, keepdims=True) + norm_eps
    inv_proj = lax.rsqrt(squared)
    unit_feat = feat_f * lax.rsqrt(jnp.sum(feat_f * feat_f, axis=-1, keepdims=True) + norm_eps)
    cosine = jnp.sum(projected * unit_feat, axis=-1, keepdims=True) * inv_proj
    return (cosine * projected / squared - unit_feat * inv_proj).astype(jnp.bfloat16)


def silu_slope(preact):
    sigma = jax.nn.sigmoid(preact)
    return sigma * (1.0 + preact * (1.0 - sigma))


def contract_rows(left, right):
    return lax.dot_general(
        left, right, (((0,), (0,)), ((), ())), preferred_element_type=jnp.float32
    )


def on_device(
    encoder_patch_input,
    encoder_norm_gains,
    encoder_input_weight,
    encoder_output_weight,
    diffuser_hidden_states,
    projector_first_weight,
    projector_second_weight,
):
    segments = lax.axis_size("segment")
    segment_pos = lax.axis_index("segment")
    token_rows = diffuser_hidden_states.shape[1]
    source = encoder_patch_input[0]
    feat_width = source.shape[1]
    scale_row = encoder_norm_gains[0]
    weight_in = encoder_input_weight[0]
    weight_out = encoder_output_weight[0]

    def run_layer(entering):
        return encoder_layer(entering, scale_row, weight_in, weight_out)

    def pass_through(entering):
        return entering

    blank = jnp.zeros((token_rows, feat_width), jnp.bfloat16)
    inbound = blank
    finished = []
    for moment in range(2 * segments - 1):
        if moment < segments:
            inject = source[moment * token_rows : (moment + 1) * token_rows]
        else:
            inject = blank
        entering = jnp.where(segment_pos == 0, inject, inbound)
        active = jnp.logical_and(segment_pos <= moment, moment - segment_pos < segments)
        leaving = lax.cond(active, run_layer, pass_through, entering)
        if moment < 2 * segments - 2:
            inbound = shifted(leaving, "segment", 1)
        if moment >= segments - 1:
            finished.append(leaving)
    stacked = jnp.concatenate(finished, axis=0)
    everything = from_root(stacked, "segment", segments - 1)
    own_feats = lax.dynamic_slice_in_dim(everything, segment_pos * token_rows, token_rows, 0)
    first_block, second_block = (
        lax.all_gather(projector_first_weight, "dp", axis=0, tiled=True),
        lax.all_gather(projector_second_weight, "dp", axis=0, tiled=True),
    )
    hidden_combined = lax.all_gather(diffuser_hidden_states[0], "segment", axis=0, tiled=True)
    preact = jnp.dot(hidden_combined, first_block, preferred_element_type=jnp.float32)
    activated = jax.nn.silu(preact).astype(jnp.bfloat16)
    projected = lax.psum_scatter(
        jnp.dot(activated, second_block, preferred_element_type=jnp.float32),
        "segment",
        scatter_dimension=0,
        tiled=True,
    )
    grad_own = cosine_grad(projected, own_feats)
    grad_all = lax.all_gather(grad_own, "segment", axis=0, tiled=True)
    grad_second = contract_rows(activated, grad_all)
    back = lax.dot_general(
        grad_all, second_block, (((1,), (1,)), ((), ())), preferred_element_type=jnp.float32
    )
    grad_pre = (back * silu_slope(preact)).astype(jnp.bfloat16)
    grad_first = contract_rows(hidden_combined, grad_pre)
    first_rows, second_rows = (
        lax.psum_scatter(grad_first, "dp", scatter_dimension=0, tiled=True),
        lax.psum_scatter(grad_second, "dp", scatter_dimension=0, tiled=True),
    )
    return (first_rows, second_rows)


def solution(mesh):
    placed = (
        P("dp", None, None),
        P("segment", None),
        P("segment", None, None),
        P("segment", None, None),
        P("dp", "segment", None),
        P("dp", "segment"),
        P(("segment", "dp"), None),
    )
    return jax.shard_map(
        on_device,
        mesh=mesh,
        in_specs=placed,
        out_specs=(P("dp", "segment"), P(("segment", "dp"), None)),
        check_vma=False,
    )
```

profile of v0, /device:TPU:2, one launch (start us, length us, event | category | flops | bytes accessed | tf_op | source)
XLA Modules:
  0.0 760.4 jit_solution(12394751905636336380)
XLA Ops:
  9.0 5.2 collective-permute-start
  14.3 7.2 collective-permute-done
  25.7 11.2 %collective-permute-done.1 = bf16[128,1024]{1,0:T(8,128)(2,1)S(1)} collective-permute-done((bf16[128,1024]{1,0:T(8,128)(2,1)S(1)}, bf16[128,1024]{1,0:T(8,128)(2,1)S(1)}, u32[]{:S(2)}, u32[]{:S(2)}) %collective-permute-start.1) | collective-permute-done | bytes 262176 | tf_op jit(solution)/shard_map/ppermute | solution.py:12
  36.9 5.3 conditional.17
  44.2 8.8 %collective-permute-done.2 = bf16[128,1024]{1,0:T(8,128)(2,1)S(1)} collective-permute-done((bf16[128,1024]{1,0:T(8,128)(2,1)S(1)}, bf16[128,1024]{1,0:T(8,128)(2,1)S(1)}, u32[]{:S(2)}, u32[]{:S(2)}) %collective-permute-start.2) | collective-permute-done | bytes 262176 | tf_op jit(solution)/shard_map/ppermute | solution.py:12
  53.1 5.3 conditional.18
  60.3 8.8 %collective-permute-done.3 = bf16[128,1024]{1,0:T(8,128)(2,1)S(1)} collective-permute-done((bf16[128,1024]{1,0:T(8,128)(2,1)S(1)}, bf16[128,1024]{1,0:T(8,128)(2,1)S(1)}, u32[]{:S(2)}, u32[]{:S(2)}) %collective-permute-start.3) | collective-permute-done | bytes 262176 | tf_op jit(solution)/shard_map/ppermute | solution.py:12
  69.2 5.3 conditional.19
  76.4 8.7 %collective-permute-done.4 = bf16[128,1024]{1,0:T(8,128)(2,1)S(1)} collective-permute-done((bf16[128,1024]{1,0:T(8,128)(2,1)S(1)}, bf16[128,1024]{1,0:T(8,128)(2,1)S(1)}, u32[]{:S(2)}, u32[]{:S(2)}) %collective-permute-start.4) | collective-permute-done | bytes 262176 | tf_op jit(solution)/shard_map/ppermute | solution.py:12
  85.2 5.3 conditional.20
  92.4 8.7 %collective-permute-done.5 = bf16[128,1024]{1,0:T(8,128)(2,1)S(1)} collective-permute-done((bf16[128,1024]{1,0:T(8,128)(2,1)S(1)}, bf16[128,1024]{1,0:T(8,128)(2,1)S(1)}, u32[]{:S(2)}, u32[]{:S(2)}) %collective-permute-start.5) | collective-permute-done | bytes 262176 | tf_op jit(solution)/shard_map/ppermute | solution.py:12
  101.2 5.5 conditional.21
  108.6 9.1 %collective-permute-done.6 = bf16[128,1024]{1,0:T(8,128)(2,1)S(1)} collective-permute-done((bf16[128,1024]{1,0:T(8,128)(2,1)S(1)}, bf16[128,1024]{1,0:T(8,128)(2,1)S(1)}, u32[]{:S(2)}, u32[]{:S(2)}) %collective-permute-start.6) | collective-permute-done | bytes 262176 | tf_op jit(solution)/shard_map/ppermute | solution.py:12
  117.7 5.3 conditional.22
  125.0 14.4 %collective-permute-done.7 = bf16[128,1024]{1,0:T(8,128)(2,1)S(1)} collective-permute-done((bf16[128,1024]{1,0:T(8,128)(2,1)S(1)}, bf16[128,1024]{1,0:T(8,128)(2,1)S(1)}, u32[]{:S(2)}, u32[]{:S(2)}) %collective-permute-start.7) | collective-permute-done | bytes 262176 | tf_op jit(solution)/shard_map/ppermute | solution.py:12
  139.4 5.3 conditional.23
  146.7 11.1 %collective-permute-done.8 = bf16[128,1024]{1,0:T(8,128)(2,1)S(1)} collective-permute-done((bf16[128,1024]{1,0:T(8,128)(2,1)S(1)}, bf16[128,1024]{1,0:T(8,128)(2,1)S(1)}, u32[]{:S(2)}, u32[]{:S(2)}) %collective-permute-start.8) | collective-permute-done | bytes 262176 | tf_op jit(solution)/shard_map/ppermute | solution.py:12
  157.8 5.3 conditional.24
  163.1 5.6 collective-permute-start.9
  168.7 8.2 %collective-permute-done.9 = bf16[128,1024]{1,0:T(8,128)(2,1)S(1)} collective-permute-done((bf16[128,1024]{1,0:T(8,128)(2,1)S(1)}, bf16[128,1024]{1,0:T(8,128)(2,1)S(1)}, u32[]{:S(2)}, u32[]{:S(2)}) %collective-permute-start.9) | collective-permute-done | bytes 262176 | tf_op jit(solution)/shard_map/ppermute | solution.py:12
  176.9 8.4 %collective-permute-start.10 = (bf16[128,1024]{1,0:T(8,128)(2,1)S(1)}, bf16[128,1024]{1,0:T(8,128)(2,1)S(1)}, u32[]{:S(2)}, u32[]{:S(2)}) collective-permute-start(bf16[128,1024]{1,0:T(8,128)(2,1)S(1)} %get-tuple-element.261), channel_id=1, source_target_pairs={{0,32},{32,64},{64,96},{96,128},{128,160},{160,192},{192,224},{1,3... | collective-permute-start | bytes 786440 | tf_op jit(solution)/shard_map/ppermute | solution.py:12
  189.3 6.2 collective-permute-start.11
  195.6 6.6 collective-permute-done.11
  203.4 9.3 %collective-permute-start.12 = (bf16[128,1024]{1,0:T(8,128)(2,1)S(1)}, bf16[128,1024]{1,0:T(8,128)(2,1)S(1)}, u32[]{:S(2)}, u32[]{:S(2)}) collective-permute-start(bf16[128,1024]{1,0:T(8,128)(2,1)S(1)} %get-tuple-element.263), channel_id=1, source_target_pairs={{0,32},{32,64},{64,96},{96,128},{128,160},{160,192},{192,224},{1,3... | collective-permute-start | bytes 786440 | tf_op jit(solution)/shard_map/ppermute | solution.py:12
  216.6 6.9 collective-permute-start.13
  229.0 32.9 %all_gather.14 = bf16[256,1024]{1,0:T(8,128)(2,1)S(1)} all-gather(bf16[8,1024]{1,0:T(8,128)(2,1)S(1)} %copy-done.2), channel_id=1, replica_groups=mesh['segment'=8,'dp'=32] {'dp'}, dimensions={0}, use_global_device_ids=true | all-gather | bytes 540672 | tf_op jit(solution)/shard_map/all_gather | solution.py:96
  268.5 91.8 %all-reduce.2.cloned.1.call-done = bf16[1024,1024]{1,0:T(8,128)(2,1)} async-done(((bf16[1024,1024]{1,0:T(8,128)(2,1)}), bf16[1024,1024]{1,0:T(8,128)(2,1)}) %all-reduce.2.cloned.1.call-update) | async-done | bytes 2097168 | tf_op jit(solution)/shard_map/psum | solution.py:17
  361.4 92.7 %reduce-scatter.6.cloned.1.call-done = f32[128,1024]{1,0:T(8,128)} async-done(((f32[1024,1024]{1,0:T(8,128)}), f32[128,1024]{1,0:T(8,128)}) %reduce-scatter.6.cloned.1.call-update) | async-done | bytes 524304 | tf_op jit(solution)/shard_map/reduce_scatter | solution.py:101
  457.5 59.0 %all-gather.7.cloned.1.call-done = bf16[1024,1024]{1,0:T(8,128)(2,1)} async-done(((bf16[128,1024]{1,0:T(8,128)(2,1)}), bf16[1024,1024]{1,0:T(8,128)(2,1)}) %all-gather.7.cloned.1.call-update) | async-done | bytes 2097168 | tf_op jit(solution)/shard_map/all_gather | solution.py:108
  520.0 6.1 fusion.469
  528.0 107.9 %reduce-scatter.8.cloned.1.call-done = f32[8,1024]{1,0:T(8,128)} async-done(((f32[256,1024]{1,0:T(8,128)}), f32[8,1024]{1,0:T(8,128)}) %reduce-scatter.8.cloned.1.call-update) | async-done | bytes 32784 | tf_op jit(solution)/shard_map/reduce_scatter | solution.py:117
  635.9 117.7 %reduce-scatter.10.cloned.1.call-done = f32[64,256]{1,0:T(8,128)} async-done(((f32[2048,256]{1,0:T(8,128)}), f32[64,256]{1,0:T(8,128)}) %reduce-scatter.10.cloned.1.call-update) | async-done | bytes 65552
  (105 shorter events, 92.7 us)
Async XLA Ops:
  7.2 254.8 %all-gather.5.cloned.1.call-start = ((), (), s32[]{:S(2)}) async-start(), calls=%async_computation.3 | async-start | bytes 1081344 | tf_op jit(solution)/shard_map/all_gather | solution.py:95
  7.9 254.0 %all-gather.9.cloned.1.call-start = ((), (), s32[]{:S(2)}) async-start(), calls=%async_computation.8 | async-start | bytes 4718592 | tf_op jit(solution)/shard_map/all_gather | solution.py:98
  8.9 12.5 %copy-start = (bf16[1,1024,1024]{2,1,0:T(8,128)(2,1)S(1)}, bf16[1,1024,1024]{2,1,0:T(8,128)(2,1)}, u32[]{:S(2)}) copy-start(bf16[1,1024,1024]{2,1,0:T(8,128)(2,1)} %param.37) | copy-start | bytes 6291460
  9.0 12.5 %collective-permute-start = (bf16[128,1024]{1,0:T(8,128)(2,1)S(1)}, bf16[128,1024]{1,0:T(8,128)(2,1)S(1)}, u32[]{:S(2)}, u32[]{:S(2)}) collective-permute-start(bf16[128,1024]{1,0:T(8,128)(2,1)S(1)} %get-tuple-element.251), channel_id=1, source_target_pairs={{0,32},{32,64},{64,96},{96,128},{128,160},{160,192},{192,224},{1,3... | collective-permute-start | bytes 786440 | tf_op jit(solution)/shard_map/ppermute | solution.py:12
  14.2 346.1 %all-reduce.2.cloned.1.call-start = ((), (), s32[]{:S(2)}) async-start(), calls=%async_computation.5 | async-start | bytes 4194304 | tf_op jit(solution)/shard_map/psum | solution.py:17
  21.5 15.4 %collective-permute-start.1 = (bf16[128,1024]{1,0:T(8,128)(2,1)S(1)}, bf16[128,1024]{1,0:T(8,128)(2,1)S(1)}, u32[]{:S(2)}, u32[]{:S(2)}) collective-permute-start(bf16[128,1024]{1,0:T(8,128)(2,1)S(1)} %get-tuple-element.252), channel_id=1, source_target_pairs={{0,32},{32,64},{64,96},{96,128},{128,160},{160,192},{192,224},{1,3... | collective-permute-start | bytes 786440 | tf_op jit(solution)/shard_map/ppermute | solution.py:12
  42.3 10.8 %collective-permute-start.2 = (bf16[128,1024]{1,0:T(8,128)(2,1)S(1)}, bf16[128,1024]{1,0:T(8,128)(2,1)S(1)}, u32[]{:S(2)}, u32[]{:S(2)}) collective-permute-start(bf16[128,1024]{1,0:T(8,128)(2,1)S(1)} %get-tuple-element.253), channel_id=1, source_target_pairs={{0,32},{32,64},{64,96},{96,128},{128,160},{160,192},{192,224},{1,3... | collective-permute-start | bytes 786440 | tf_op jit(solution)/shard_map/ppermute | solution.py:12
  58.4 10.8 %collective-permute-start.3 = (bf16[128,1024]{1,0:T(8,128)(2,1)S(1)}, bf16[128,1024]{1,0:T(8,128)(2,1)S(1)}, u32[]{:S(2)}, u32[]{:S(2)}) collective-permute-start(bf16[128,1024]{1,0:T(8,128)(2,1)S(1)} %get-tuple-element.254), channel_id=1, source_target_pairs={{0,32},{32,64},{64,96},{96,128},{128,160},{160,192},{192,224},{1,3... | collective-permute-start | bytes 786440 | tf_op jit(solution)/shard_map/ppermute | solution.py:12
  74.5 10.7 %collective-permute-start.4 = (bf16[128,1024]{1,0:T(8,128)(2,1)S(1)}, bf16[128,1024]{1,0:T(8,128)(2,1)S(1)}, u32[]{:S(2)}, u32[]{:S(2)}) collective-permute-start(bf16[128,1024]{1,0:T(8,128)(2,1)S(1)} %get-tuple-element.255), channel_id=1, source_target_pairs={{0,32},{32,64},{64,96},{96,128},{128,160},{160,192},{192,224},{1,3... | collective-permute-start | bytes 786440 | tf_op jit(solution)/shard_map/ppermute | solution.py:12
  90.5 10.7 %collective-permute-start.5 = (bf16[128,1024]{1,0:T(8,128)(2,1)S(1)}, bf16[128,1024]{1,0:T(8,128)(2,1)S(1)}, u32[]{:S(2)}, u32[]{:S(2)}) collective-permute-start(bf16[128,1024]{1,0:T(8,128)(2,1)S(1)} %get-tuple-element.256), channel_id=1, source_target_pairs={{0,32},{32,64},{64,96},{96,128},{128,160},{160,192},{192,224},{1,3... | collective-permute-start | bytes 786440 | tf_op jit(solution)/shard_map/ppermute | solution.py:12
  106.7 11.0 %collective-permute-start.6 = (bf16[128,1024]{1,0:T(8,128)(2,1)S(1)}, bf16[128,1024]{1,0:T(8,128)(2,1)S(1)}, u32[]{:S(2)}, u32[]{:S(2)}) collective-permute-start(bf16[128,1024]{1,0:T(8,128)(2,1)S(1)} %get-tuple-element.257), channel_id=1, source_target_pairs={{0,32},{32,64},{64,96},{96,128},{128,160},{160,192},{192,224},{1,3... | collective-permute-start | bytes 786440 | tf_op jit(solution)/shard_map/ppermute | solution.py:12
  123.0 16.3 %collective-permute-start.7 = (bf16[128,1024]{1,0:T(8,128)(2,1)S(1)}, bf16[128,1024]{1,0:T(8,128)(2,1)S(1)}, u32[]{:S(2)}, u32[]{:S(2)}) collective-permute-start(bf16[128,1024]{1,0:T(8,128)(2,1)S(1)} %get-tuple-element.258), channel_id=1, source_target_pairs={{0,32},{32,64},{64,96},{96,128},{128,160},{160,192},{192,224},{1,3... | collective-permute-start | bytes 786440 | tf_op jit(solution)/shard_map/ppermute | solution.py:12
  144.7 13.0 %collective-permute-start.8 = (bf16[128,1024]{1,0:T(8,128)(2,1)S(1)}, bf16[128,1024]{1,0:T(8,128)(2,1)S(1)}, u32[]{:S(2)}, u32[]{:S(2)}) collective-permute-start(bf16[128,1024]{1,0:T(8,128)(2,1)S(1)} %get-tuple-element.259), channel_id=1, source_target_pairs={{0,32},{32,64},{64,96},{96,128},{128,160},{160,192},{192,224},{1,3... | collective-permute-start | bytes 786440 | tf_op jit(solution)/shard_map/ppermute | solution.py:12
  163.1 13.8 %collective-permute-start.9 = (bf16[128,1024]{1,0:T(8,128)(2,1)S(1)}, bf16[128,1024]{1,0:T(8,128)(2,1)S(1)}, u32[]{:S(2)}, u32[]{:S(2)}) collective-permute-start(bf16[128,1024]{1,0:T(8,128)(2,1)S(1)} %get-tuple-element.260), channel_id=1, source_target_pairs={{0,32},{32,64},{64,96},{96,128},{128,160},{160,192},{192,224},{1,3... | collective-permute-start | bytes 786440 | tf_op jit(solution)/shard_map/ppermute | solution.py:12
  176.9 12.3 %collective-permute-start.10 = (bf16[128,1024]{1,0:T(8,128)(2,1)S(1)}, bf16[128,1024]{1,0:T(8,128)(2,1)S(1)}, u32[]{:S(2)}, u32[]{:S(2)}) collective-permute-start(bf16[128,1024]{1,0:T(8,128)(2,1)S(1)} %get-tuple-element.261), channel_id=1, source_target_pairs={{0,32},{32,64},{64,96},{96,128},{128,160},{160,192},{192,224},{1,3... | collective-permute-start | bytes 786440 | tf_op jit(solution)/shard_map/ppermute | solution.py:12
  189.3 12.8 %collective-permute-start.11 = (bf16[128,1024]{1,0:T(8,128)(2,1)S(1)}, bf16[128,1024]{1,0:T(8,128)(2,1)}, u32[]{:S(2)}, u32[]{:S(2)}) collective-permute-start(bf16[128,1024]{1,0:T(8,128)(2,1)S(1)} %get-tuple-element.262), channel_id=1, source_target_pairs={{0,32},{32,64},{64,96},{96,128},{128,160},{160,192},{192,224},{1,3... | collective-permute-start | bytes 786440 | tf_op jit(solution)/shard_map/ppermute | solution.py:12
  203.4 13.2 %collective-permute-start.12 = (bf16[128,1024]{1,0:T(8,128)(2,1)S(1)}, bf16[128,1024]{1,0:T(8,128)(2,1)S(1)}, u32[]{:S(2)}, u32[]{:S(2)}) collective-permute-start(bf16[128,1024]{1,0:T(8,128)(2,1)S(1)} %get-tuple-element.263), channel_id=1, source_target_pairs={{0,32},{32,64},{64,96},{96,128},{128,160},{160,192},{192,224},{1,3... | collective-permute-start | bytes 786440 | tf_op jit(solution)/shard_map/ppermute | solution.py:12
  216.6 10.8 %collective-permute-start.13 = (bf16[128,1024]{1,0:T(8,128)(2,1)S(1)}, bf16[128,1024]{1,0:T(8,128)(2,1)S(1)}, u32[]{:S(2)}, u32[]{:S(2)}) collective-permute-start(bf16[128,1024]{1,0:T(8,128)(2,1)S(1)} %get-tuple-element.264), channel_id=1, source_target_pairs={{0,32},{32,64},{64,96},{96,128},{128,160},{160,192},{192,224},{1,3... | collective-permute-start | bytes 786440 | tf_op jit(solution)/shard_map/ppermute | solution.py:12
  227.4 1.6 copy-start.2
  229.0 225.1 %reduce-scatter.6.cloned.1.call-start = ((), (), s32[]{:S(2)}) async-start(), calls=%async_computation.4 | async-start | bytes 4718592 | tf_op jit(solution)/shard_map/reduce_scatter | solution.py:101
  265.7 250.9 %copy-start.3 = (f32[1024,256]{1,0:T(8,128)}, f32[1024,256]{1,0:T(8,128)S(1)}, u32[]{:S(2)}) copy-start(f32[1024,256]{1,0:T(8,128)S(1)} %fusion.467) | copy-start | bytes 3145732
  268.4 248.1 %all-gather.7.cloned.1.call-start = ((), (), s32[]{:S(2)}) async-start(), calls=%async_computation.6 | async-start | bytes 2359296 | tf_op jit(solution)/shard_map/all_gather | solution.py:108
  457.5 178.4 %reduce-scatter.8.cloned.1.call-start = ((), (), s32[]{:S(2)}) async-start(), calls=%async_computation.7 | async-start | bytes 1081344 | tf_op jit(solution)/shard_map/reduce_scatter | solution.py:117
  519.9 233.6 %reduce-scatter.10.cloned.1.call-start = ((), (), s32[]{:S(2)}) async-start(), calls=%async_computation.9 | async-start | bytes 2162688
Sparse Core Ops, SparseCore 0:
  9.8 66.5 all-gather.4
  79.1 94.0 all-gather.8
  229.1 131.1 all-reduce.1
  364.3 89.7 reduce-scatter.5
  457.6 58.9 all-gather.6
  520.1 115.7 reduce-scatter.7
  639.1 114.3 reduce-scatter.9
where the time goes:
time: 761 us; the launch traced here: 760 us
  waiting for transfers between devices  584 us (77%)
  starting transfers between devices  59.6 us (8%)
  matrix products  56.8 us (7%)
  blocking collectives  32.9 us (4%)
  between operations  14.6 us (2%)
  other arithmetic  9.31 us (1%)
    unnamed x8, waiting for transfers between devices  118 us
    ppermute x14, waiting for transfers between devices, shifted(): return lax.ppermute(block, axis, route)  114 us
    reduce_scatter x1, waiting for transfers between devices, on_device(): lax.psum_scatter(grad_second, 'dp', scatter_dimension=0, tiled=True)  108 us
    reduce_scatter x1, waiting for transfers between devices, on_device(): lax.psum_scatter(jnp.dot(activated, second_block, preferred_element_type=...  92.7 us
    psum x1, waiting for transfers between devices, from_root(): return lax.psum(block, axis)  91.8 us
    ppermute x14, starting transfers between devices, shifted(): return lax.ppermute(block, axis, route)  59.4 us
    all_gather x1, waiting for transfers between devices, on_device(): grad_all = lax.all_gather(grad_own, 'segment', axis=0, tiled=True)  59 us
    dot_general x8, matrix products, encoder_layer(): jnp.dot(inner, weight_out, preferred_element_type=jnp.float32)  40.9 us
  transfers between devices with their start and end apart: 21, of which 19 were waited for; matrix products, arithmetic and copies ran while one was open for 8% of the time, Pallas kernels for 0%

commit v1 on v0

--- a/solution.py
+++ b/solution.py
@@ -4,6 +4,12 @@
 from jax.sharding import PartitionSpec as P
 
 norm_eps = 1e-06
+
+
+def gather_and_add(x, axis):
+    parts = lax.all_gather(x, axis, axis=0, tiled=False)
+    total = parts.sum(axis=0)
+    return total
 
 
 def shifted(block, axis, distance):
@@ -14,7 +20,7 @@
 
 def from_root(block, axis, holder):
     block = jnp.where(lax.axis_index(axis) == holder, block, jnp.zeros_like(block))
-    return lax.psum(block, axis)
+    return gather_and_add(block, axis)
 
 
 def encoder_layer(hidden, scale_row, weight_in, weight_out):

time: 761 us -> 834 us (1.096)
  waiting for transfers between devices: 584 us -> 647 us
    all_gather x0 -> x1, waiting for transfers between devices: none -> 165 us  [gather_and_add(): parts = lax.all_gather(x, axis, axis=0, tiled=False)]
    psum x1 -> x0, waiting for transfers between devices: 91.8 us -> none  [from_root(): return lax.psum(block, axis)]
    reduce_scatter x1, waiting for transfers between devices: 92.7 us -> 83.2 us  [on_device(): lax.psum_scatter(jnp.dot(activated, second_block, preferred_element_type=...]
    reduce_sum x0 -> x1, other arithmetic: none -> 9.46 us  [gather_and_add(): total = parts.sum(axis=0)]
where the time goes in v1:
time: 834 us; the launch traced here: 833 us
  waiting for transfers between devices  647 us (78%)
  starting transfers between devices  60.6 us (7%)
  matrix products  57.1 us (7%)
  blocking collectives  33.7 us (4%)
  other arithmetic  16.8 us (2%)
  between operations  14.6 us (2%)
    all_gather x1, waiting for transfers between devices, gather_and_add(): parts = lax.all_gather(x, axis, axis=0, tiled=False)  165 us
    unnamed x8, waiting for transfers between devices  118 us
    ppermute x14, waiting for transfers between devices, shifted(): return lax.ppermute(block, axis, route)  114 us
    reduce_scatter x1, waiting for transfers between devices, on_device(): lax.psum_scatter(grad_second, 'dp', scatter_dimension=0, tiled=True)  108 us
    reduce_scatter x1, waiting for transfers between devices, on_device(): lax.psum_scatter(jnp.dot(activated, second_block, preferred_element_type=...  83.2 us
    ppermute x14, starting transfers between devices, shifted(): return lax.ppermute(block, axis, route)  60 us
    all_gather x1, waiting for transfers between devices, on_device(): grad_all = lax.all_gather(grad_own, 'segment', axis=0, tiled=True)  59 us
    dot_general x8, matrix products, encoder_layer(): jnp.dot(inner, weight_out, preferred_element_type=jnp.float32)  40.9 us
  transfers between devices with their start and end apart: 21, of which 19 were waited for; matrix products, arithmetic and copies ran while one was open for 8% of the time, Pallas kernels for 0%

profile of v1, /device:TPU:2, one launch (start us, length us, event | category | flops | bytes accessed | tf_op | source)
XLA Modules:
  0.0 833.3 jit_solution(4074723447263147708)
XLA Ops:
  14.2 7.2 collective-permute-done
  25.8 11.1 %collective-permute-done.1 = bf16[128,1024]{1,0:T(8,128)(2,1)S(1)} collective-permute-done((bf16[128,1024]{1,0:T(8,128)(2,1)S(1)}, bf16[128,1024]{1,0:T(8,128)(2,1)S(1)}, u32[]{:S(2)}, u32[]{:S(2)}) %collective-permute-start.1) | collective-permute-done | bytes 262176 | tf_op jit(solution)/shard_map/ppermute | solution.py:18
  36.9 5.3 conditional.17
  44.2 8.8 %collective-permute-done.2 = bf16[128,1024]{1,0:T(8,128)(2,1)S(1)} collective-permute-done((bf16[128,1024]{1,0:T(8,128)(2,1)S(1)}, bf16[128,1024]{1,0:T(8,128)(2,1)S(1)}, u32[]{:S(2)}, u32[]{:S(2)}) %collective-permute-start.2) | collective-permute-done | bytes 262176 | tf_op jit(solution)/shard_map/ppermute | solution.py:18
  53.1 5.3 conditional.18
  60.3 8.8 %collective-permute-done.3 = bf16[128,1024]{1,0:T(8,128)(2,1)S(1)} collective-permute-done((bf16[128,1024]{1,0:T(8,128)(2,1)S(1)}, bf16[128,1024]{1,0:T(8,128)(2,1)S(1)}, u32[]{:S(2)}, u32[]{:S(2)}) %collective-permute-start.3) | collective-permute-done | bytes 262176 | tf_op jit(solution)/shard_map/ppermute | solution.py:18
  69.2 5.3 conditional.19
  76.4 8.7 %collective-permute-done.4 = bf16[128,1024]{1,0:T(8,128)(2,1)S(1)} collective-permute-done((bf16[128,1024]{1,0:T(8,128)(2,1)S(1)}, bf16[128,1024]{1,0:T(8,128)(2,1)S(1)}, u32[]{:S(2)}, u32[]{:S(2)}) %collective-permute-start.4) | collective-permute-done | bytes 262176 | tf_op jit(solution)/shard_map/ppermute | solution.py:18
  85.2 5.3 conditional.20
  92.4 8.7 %collective-permute-done.5 = bf16[128,1024]{1,0:T(8,128)(2,1)S(1)} collective-permute-done((bf16[128,1024]{1,0:T(8,128)(2,1)S(1)}, bf16[128,1024]{1,0:T(8,128)(2,1)S(1)}, u32[]{:S(2)}, u32[]{:S(2)}) %collective-permute-start.5) | collective-permute-done | bytes 262176 | tf_op jit(solution)/shard_map/ppermute | solution.py:18
  101.2 5.5 conditional.21
  108.6 9.1 %collective-permute-done.6 = bf16[128,1024]{1,0:T(8,128)(2,1)S(1)} collective-permute-done((bf16[128,1024]{1,0:T(8,128)(2,1)S(1)}, bf16[128,1024]{1,0:T(8,128)(2,1)S(1)}, u32[]{:S(2)}, u32[]{:S(2)}) %collective-permute-start.6) | collective-permute-done | bytes 262176 | tf_op jit(solution)/shard_map/ppermute | solution.py:18
  117.7 5.3 conditional.22
  125.0 14.4 %collective-permute-done.7 = bf16[128,1024]{1,0:T(8,128)(2,1)S(1)} collective-permute-done((bf16[128,1024]{1,0:T(8,128)(2,1)S(1)}, bf16[128,1024]{1,0:T(8,128)(2,1)S(1)}, u32[]{:S(2)}, u32[]{:S(2)}) %collective-permute-start.7) | collective-permute-done | bytes 262176 | tf_op jit(solution)/shard_map/ppermute | solution.py:18
  139.4 5.3 conditional.23
  146.7 11.1 %collective-permute-done.8 = bf16[128,1024]{1,0:T(8,128)(2,1)S(1)} collective-permute-done((bf16[128,1024]{1,0:T(8,128)(2,1)S(1)}, bf16[128,1024]{1,0:T(8,128)(2,1)S(1)}, u32[]{:S(2)}, u32[]{:S(2)}) %collective-permute-start.8) | collective-permute-done | bytes 262176 | tf_op jit(solution)/shard_map/ppermute | solution.py:18
  157.8 5.3 conditional.24
  163.1 5.6 collective-permute-start.9
  168.7 8.2 collective-permute-done.9
  176.9 8.4 %collective-permute-start.10 = (bf16[128,1024]{1,0:T(8,128)(2,1)S(1)}, bf16[128,1024]{1,0:T(8,128)(2,1)S(1)}, u32[]{:S(2)}, u32[]{:S(2)}) collective-permute-start(bf16[128,1024]{1,0:T(8,128)(2,1)S(1)} %get-tuple-element.316), channel_id=1, source_target_pairs={{0,32},{32,64},{64,96},{96,128},{128,160},{160,192},{192,224},{1,3... | collective-permute-start | bytes 786440 | tf_op jit(solution)/shard_map/ppermute | solution.py:18
  189.3 6.2 collective-permute-start.11
  195.6 5.7 collective-permute-done.11
  201.6 10.1 %collective-permute-start.12 = (bf16[128,1024]{1,0:T(8,128)(2,1)S(1)}, bf16[128,1024]{1,0:T(8,128)(2,1)S(1)}, u32[]{:S(2)}, u32[]{:S(2)}) collective-permute-start(bf16[128,1024]{1,0:T(8,128)(2,1)S(1)} %get-tuple-element.318), channel_id=1, source_target_pairs={{0,32},{32,64},{64,96},{96,128},{128,160},{160,192},{192,224},{1,3... | collective-permute-start | bytes 786440 | tf_op jit(solution)/shard_map/ppermute | solution.py:18
  215.7 6.8 collective-permute-start.13
  228.0 33.7 %all_gather.18 = bf16[256,1024]{1,0:T(8,128)(2,1)S(1)} all-gather(bf16[8,1024]{1,0:T(8,128)(2,1)S(1)} %copy-done.1), channel_id=1, replica_groups=mesh['segment'=8,'dp'=32] {'dp'}, dimensions={0}, use_global_device_ids=true | all-gather | bytes 540672 | tf_op jit(solution)/shard_map/all_gather | solution.py:102
  269.3 164.8 %all-gather.8.cloned.1.call-done = bf16[8,1024,1024]{2,1,0:T(8,128)(2,1)} async-done(((bf16[1,1024,1024]{2,1,0:T(8,128)(2,1)}), bf16[8,1024,1024]{2,1,0:T(8,128)(2,1)}) %all-gather.8.cloned.1.call-update) | async-done | bytes 16777232 | tf_op jit(solution)/shard_map/all_gather | solution.py:10
  434.0 9.5 %reduce_sum.174 = bf16[1024,1024]{1,0:T(8,128)(2,1)S(1)} reduce(bf16[8,1024,1024]{2,1,0:T(8,128)(2,1)} %all-gather.8.cloned.1.call-done, bf16[]{:T(256)} %constant.266.clone.1), dimensions={0}, to_apply=%region_46.47 | reduce | flops 7340032 | bytes 18874370 | tf_op jit(solution)/shard_map/reduce_sum | solution.py:11
  443.6 83.2 %reduce-scatter.6.cloned.1.call-done = f32[128,1024]{1,0:T(8,128)} async-done(((f32[1024,1024]{1,0:T(8,128)}), f32[128,1024]{1,0:T(8,128)}) %reduce-scatter.6.cloned.1.call-update) | async-done | bytes 524304 | tf_op jit(solution)/shard_map/reduce_scatter | solution.py:107
  530.1 59.0 %all-gather.10.cloned.1.call-done = bf16[1024,1024]{1,0:T(8,128)(2,1)} async-done(((bf16[128,1024]{1,0:T(8,128)(2,1)}), bf16[1024,1024]{1,0:T(8,128)(2,1)}) %all-gather.10.cloned.1.call-update) | async-done | bytes 2097168 | tf_op jit(solution)/shard_map/all_gather | solution.py:114
  593.1 6.1 fusion.470
  601.1 107.7 %reduce-scatter.8.cloned.1.call-done = f32[8,1024]{1,0:T(8,128)} async-done(((f32[256,1024]{1,0:T(8,128)}), f32[8,1024]{1,0:T(8,128)}) %reduce-scatter.8.cloned.1.call-update) | async-done | bytes 32784 | tf_op jit(solution)/shard_map/reduce_scatter | solution.py:123
  708.8 117.7 %reduce-scatter.10.cloned.1.call-done = f32[64,256]{1,0:T(8,128)} async-done(((f32[2048,256]{1,0:T(8,128)}), f32[64,256]{1,0:T(8,128)}) %reduce-scatter.10.cloned.1.call-update) | async-done | bytes 65552
  (107 shorter events, 97.5 us)
Async XLA Ops:
  7.2 254.6 %all-gather.6.cloned.1.call-start = ((), (), s32[]{:S(2)}) async-start(), calls=%async_computation.3 | async-start | bytes 1081344 | tf_op jit(solution)/shard_map/all_gather | solution.py:101
  7.9 253.9 %all-gather.12.cloned.1.call-start = ((), (), s32[]{:S(2)}) async-start(), calls=%async_computation.8 | async-start | bytes 4718592 | tf_op jit(solution)/shard_map/all_gather | solution.py:104
  8.9 12.5 %copy-start = (bf16[1,1024,1024]{2,1,0:T(8,128)(2,1)S(1)}, bf16[1,1024,1024]{2,1,0:T(8,128)(2,1)}, u32[]{:S(2)}) copy-start(bf16[1,1024,1024]{2,1,0:T(8,128)(2,1)} %param.37) | copy-start | bytes 6291460
  9.0 12.5 %collective-permute-start = (bf16[128,1024]{1,0:T(8,128)(2,1)S(1)}, bf16[128,1024]{1,0:T(8,128)(2,1)S(1)}, u32[]{:S(2)}, u32[]{:S(2)}) collective-permute-start(bf16[128,1024]{1,0:T(8,128)(2,1)S(1)} %get-tuple-element.306), channel_id=1, source_target_pairs={{0,32},{32,64},{64,96},{96,128},{128,160},{160,192},{192,224},{1,3... | collective-permute-start | bytes 786440 | tf_op jit(solution)/shard_map/ppermute | solution.py:18
  21.5 15.4 %collective-permute-start.1 = (bf16[128,1024]{1,0:T(8,128)(2,1)S(1)}, bf16[128,1024]{1,0:T(8,128)(2,1)S(1)}, u32[]{:S(2)}, u32[]{:S(2)}) collective-permute-start(bf16[128,1024]{1,0:T(8,128)(2,1)S(1)} %get-tuple-element.307), channel_id=1, source_target_pairs={{0,32},{32,64},{64,96},{96,128},{128,160},{160,192},{192,224},{1,3... | collective-permute-start | bytes 786440 | tf_op jit(solution)/shard_map/ppermute | solution.py:18
  25.7 408.3 %all-gather.8.cloned.1.call-start = ((), (), s32[]{:S(2)}) async-start(), calls=%async_computation.5 | async-start | bytes 18874368 | tf_op jit(solution)/shard_map/all_gather | solution.py:10
  42.3 10.8 %collective-permute-start.2 = (bf16[128,1024]{1,0:T(8,128)(2,1)S(1)}, bf16[128,1024]{1,0:T(8,128)(2,1)S(1)}, u32[]{:S(2)}, u32[]{:S(2)}) collective-permute-start(bf16[128,1024]{1,0:T(8,128)(2,1)S(1)} %get-tuple-element.308), channel_id=1, source_target_pairs={{0,32},{32,64},{64,96},{96,128},{128,160},{160,192},{192,224},{1,3... | collective-permute-start | bytes 786440 | tf_op jit(solution)/shard_map/ppermute | solution.py:18
  58.4 10.8 %collective-permute-start.3 = (bf16[128,1024]{1,0:T(8,128)(2,1)S(1)}, bf16[128,1024]{1,0:T(8,128)(2,1)S(1)}, u32[]{:S(2)}, u32[]{:S(2)}) collective-permute-start(bf16[128,1024]{1,0:T(8,128)(2,1)S(1)} %get-tuple-element.309), channel_id=1, source_target_pairs={{0,32},{32,64},{64,96},{96,128},{128,160},{160,192},{192,224},{1,3... | collective-permute-start | bytes 786440 | tf_op jit(solution)/shard_map/ppermute | solution.py:18
  74.5 10.7 %collective-permute-start.4 = (bf16[128,1024]{1,0:T(8,128)(2,1)S(1)}, bf16[128,1024]{1,0:T(8,128)(2,1)S(1)}, u32[]{:S(2)}, u32[]{:S(2)}) collective-permute-start(bf16[128,1024]{1,0:T(8,128)(2,1)S(1)} %get-tuple-element.310), channel_id=1, source_target_pairs={{0,32},{32,64},{64,96},{96,128},{128,160},{160,192},{192,224},{1,3... | collective-permute-start | bytes 786440 | tf_op jit(solution)/shard_map/ppermute | solution.py:18
  90.5 10.7 %collective-permute-start.5 = (bf16[128,1024]{1,0:T(8,128)(2,1)S(1)}, bf16[128,1024]{1,0:T(8,128)(2,1)S(1)}, u32[]{:S(2)}, u32[]{:S(2)}) collective-permute-start(bf16[128,1024]{1,0:T(8,128)(2,1)S(1)} %get-tuple-element.311), channel_id=1, source_target_pairs={{0,32},{32,64},{64,96},{96,128},{128,160},{160,192},{192,224},{1,3... | collective-permute-start | bytes 786440 | tf_op jit(solution)/shard_map/ppermute | solution.py:18
  106.7 11.0 %collective-permute-start.6 = (bf16[128,1024]{1,0:T(8,128)(2,1)S(1)}, bf16[128,1024]{1,0:T(8,128)(2,1)S(1)}, u32[]{:S(2)}, u32[]{:S(2)}) collective-permute-start(bf16[128,1024]{1,0:T(8,128)(2,1)S(1)} %get-tuple-element.312), channel_id=1, source_target_pairs={{0,32},{32,64},{64,96},{96,128},{128,160},{160,192},{192,224},{1,3... | collective-permute-start | bytes 786440 | tf_op jit(solution)/shard_map/ppermute | solution.py:18
  123.0 16.3 %collective-permute-start.7 = (bf16[128,1024]{1,0:T(8,128)(2,1)S(1)}, bf16[128,1024]{1,0:T(8,128)(2,1)S(1)}, u32[]{:S(2)}, u32[]{:S(2)}) collective-permute-start(bf16[128,1024]{1,0:T(8,128)(2,1)S(1)} %get-tuple-element.313), channel_id=1, source_target_pairs={{0,32},{32,64},{64,96},{96,128},{128,160},{160,192},{192,224},{1,3... | collective-permute-start | bytes 786440 | tf_op jit(solution)/shard_map/ppermute | solution.py:18
  144.7 13.0 %collective-permute-start.8 = (bf16[128,1024]{1,0:T(8,128)(2,1)S(1)}, bf16[128,1024]{1,0:T(8,128)(2,1)S(1)}, u32[]{:S(2)}, u32[]{:S(2)}) collective-permute-start(bf16[128,1024]{1,0:T(8,128)(2,1)S(1)} %get-tuple-element.314), channel_id=1, source_target_pairs={{0,32},{32,64},{64,96},{96,128},{128,160},{160,192},{192,224},{1,3... | collective-permute-start | bytes 786440 | tf_op jit(solution)/shard_map/ppermute | solution.py:18
  163.1 13.8 %collective-permute-start.9 = (bf16[128,1024]{1,0:T(8,128)(2,1)S(1)}, bf16[128,1024]{1,0:T(8,128)(2,1)S(1)}, u32[]{:S(2)}, u32[]{:S(2)}) collective-permute-start(bf16[128,1024]{1,0:T(8,128)(2,1)S(1)} %get-tuple-element.315), channel_id=1, source_target_pairs={{0,32},{32,64},{64,96},{96,128},{128,160},{160,192},{192,224},{1,3... | collective-permute-start | bytes 786440 | tf_op jit(solution)/shard_map/ppermute | solution.py:18
  176.9 12.3 %collective-permute-start.10 = (bf16[128,1024]{1,0:T(8,128)(2,1)S(1)}, bf16[128,1024]{1,0:T(8,128)(2,1)S(1)}, u32[]{:S(2)}, u32[]{:S(2)}) collective-permute-start(bf16[128,1024]{1,0:T(8,128)(2,1)S(1)} %get-tuple-element.316), channel_id=1, source_target_pairs={{0,32},{32,64},{64,96},{96,128},{128,160},{160,192},{192,224},{1,3... | collective-permute-start | bytes 786440 | tf_op jit(solution)/shard_map/ppermute | solution.py:18
  189.3 12.0 %collective-permute-start.11 = (bf16[128,1024]{1,0:T(8,128)(2,1)S(1)}, bf16[128,1024]{1,0:T(8,128)(2,1)S(1)}, u32[]{:S(2)}, u32[]{:S(2)}) collective-permute-start(bf16[128,1024]{1,0:T(8,128)(2,1)S(1)} %get-tuple-element.317), channel_id=1, source_target_pairs={{0,32},{32,64},{64,96},{96,128},{128,160},{160,192},{192,224},{1,3... | collective-permute-start | bytes 786440 | tf_op jit(solution)/shard_map/ppermute | solution.py:18
  201.6 14.0 %collective-permute-start.12 = (bf16[128,1024]{1,0:T(8,128)(2,1)S(1)}, bf16[128,1024]{1,0:T(8,128)(2,1)S(1)}, u32[]{:S(2)}, u32[]{:S(2)}) collective-permute-start(bf16[128,1024]{1,0:T(8,128)(2,1)S(1)} %get-tuple-element.318), channel_id=1, source_target_pairs={{0,32},{32,64},{64,96},{96,128},{128,160},{160,192},{192,224},{1,3... | collective-permute-start | bytes 786440 | tf_op jit(solution)/shard_map/ppermute | solution.py:18
  215.7 10.7 %collective-permute-start.13 = (bf16[128,1024]{1,0:T(8,128)(2,1)S(1)}, bf16[128,1024]{1,0:T(8,128)(2,1)S(1)}, u32[]{:S(2)}, u32[]{:S(2)}) collective-permute-start(bf16[128,1024]{1,0:T(8,128)(2,1)S(1)} %get-tuple-element.319), channel_id=1, source_target_pairs={{0,32},{32,64},{64,96},{96,128},{128,160},{160,192},{192,224},{1,3... | collective-permute-start | bytes 786440 | tf_op jit(solution)/shard_map/ppermute | solution.py:18
  226.4 1.6 copy-start.1
  227.9 298.9 %reduce-scatter.6.cloned.1.call-start = ((), (), s32[]{:S(2)}) async-start(), calls=%async_computation.4 | async-start | bytes 4718592 | tf_op jit(solution)/shard_map/reduce_scatter | solution.py:107
  265.5 1.0 copy-start.2
  269.2 319.9 %all-gather.10.cloned.1.call-start = ((), (), s32[]{:S(2)}) async-start(), calls=%async_computation.6 | async-start | bytes 2359296 | tf_op jit(solution)/shard_map/all_gather | solution.py:114
  530.0 178.7 %reduce-scatter.8.cloned.1.call-start = ((), (), s32[]{:S(2)}) async-start(), calls=%async_computation.7 | async-start | bytes 1081344 | tf_op jit(solution)/shard_map/reduce_scatter | solution.py:123
  592.8 233.6 %reduce-scatter.10.cloned.1.call-start = ((), (), s32[]{:S(2)}) async-start(), calls=%async_computation.9 | async-start | bytes 2162688
Sparse Core Ops, SparseCore 0:
  9.8 66.5 all-gather.5
  79.1 94.0 all-gather.11
  228.1 205.9 all-gather.7
  438.0 88.7 reduce-scatter.5
  530.2 58.9 all-gather.9
  593.0 115.7 reduce-scatter.7
  712.0 114.3 reduce-scatter.9
